TPU v7x, 256 devices: a whole 4x4x8 slice. The times are simulated.
256 devices in a mesh: dp: 64 (over z, y, core), comp: 4 (over x).
Axes of the slice: x: 4, y: 4, z: 8, core: 2. Of those that a mesh axis runs over, the one named last changes fastest.
Arguments:
- points: float32 [65536, 128], P('dp'), may hold values from -64 to 64
- block_counts: int32 [64], replicated, may hold values from 1 to 16, as said below
- block_dest: int32 [64, 16], replicated, may hold values from 0 to 63, as said below
- means: float32 [256, 128], P(('dp', 'comp')), may hold values from -3 to 3
- factors: float32 [256, 128, 128], P(('dp', 'comp')), may hold values from -0.25 to 1.4, as said below
- log_weights: float32 [256], P(('dp', 'comp')), may hold values from -4 to 4
Outputs:
- new_means: float32 [256, 128], P(('dp', 'comp'))
- new_factors: float32 [256, 128, 128], P(('dp', 'comp'))
- new_log_weights: float32 [256], P(('dp', 'comp'))
- log_density: float32 [16384], P('dp')
Inputs may be any that keep to these rules, and one draw needn't show every extreme that they name: `block_counts`: blocks live on each index of dp on entry; they sum to 256, and one index holds exactly 16. `block_dest`: for j < block_counts[s], the index of dp that receives block j of index s; every index receives exactly 4 blocks, no index sends more than 1 block to one index, and some index sends exactly 1 to one; entries with j >= block_counts[s] are unused. `factors`: each matrix is upper triangular with diagonal entries from 0.7 to 1.4.
All inputs are finite; a program needn't handle non-finite values.
Results may differ from a plain program's by a relative error of at most 0.003.
Values sent between devices are 32-bit elements; how exact they have to be, the bound alone decides.
A program may use at most 128 MiB of HBM per device.

v0:
```python
import math
import jax
import jax.numpy as jnp
from jax import lax
from jax.sharding import Mesh
from jax.sharding import PartitionSpec as P

K = 256
RB = 4
ITERS = 2
DP = ("dp_0", "dp_1", "dp_2")
DP_COMP = ("dp_0", "dp_1", "dp_2", "comp")
highest = lax.Precision.HIGHEST
ridge_term = 1.0
log_two_pi = math.log(2.0 * math.pi)


def laid_out(pieces, dim):
    pieces = jnp.moveaxis(pieces, 0, dim)
    dims = pieces.shape
    return pieces.reshape(*dims[:dim], dims[dim] * dims[dim + 1], *dims[dim + 2 :])


def stacked_from(value, axes, sequence):
    pieces = value[None]
    for k in sequence:
        pieces = lax.all_gather(pieces, axes[k], axis=0, tiled=True)
    block = [lax.axis_size(axes[k]) for k in reversed(sequence)]
    pieces = pieces.reshape(*block, *value.shape)
    turned = sorted(range(len(sequence)), key=lambda place: sequence[len(sequence) - 1 - place])
    return pieces.transpose(*turned, *range(len(sequence), pieces.ndim)).reshape(-1, *value.shape)


def gathered_by_axis(value, axes, sequence, dim):
    return laid_out(stacked_from(value, axes, sequence), dim)


def copy_for_each(value, axis):
    copies = jnp.broadcast_to(value, (lax.axis_size(axis), *value.shape))
    return lax.all_to_all(copies, axis, split_axis=0, concat_axis=0, tiled=True)


def gathered_once(value, axis):
    leaves = jax.tree.leaves(value)
    sequence = sorted(range(len(leaves)), key=lambda k: -leaves[k].size)
    width = (1, *leaves[sequence[0]].shape)[-1]
    lines = [
        jnp.pad(leaves[k].reshape(-1), (0, -leaves[k].size % width)).reshape(-1, width)
        for k in sequence
    ]
    both, at, found = (copy_for_each(jnp.concatenate(lines), axis), 0, {})
    for k, line in zip(sequence, lines):
        piece = both[:, at : at + len(line)].reshape(len(both), -1)
        found[k] = piece[:, : leaves[k].size].reshape(-1, *leaves[k].shape)
        at += len(line)
    numbers = iter(range(len(leaves)))
    return jax.tree.map(lambda _: found[next(numbers)], value)


def combined_pairwise(pieces, combine):
    while len(jax.tree.leaves(pieces)[0]) > 1:
        pieces = jax.vmap(combine)(
            *(jax.tree.map(lambda part: part[side::2], pieces) for side in (0, 1))
        )
    return jax.tree.map(lambda part: part[0], pieces)


def merged(value, axis, combine):
    pieces = gathered_once(value, axis)
    return combined_pairwise(pieces, combine)


def in_blocks(value, dim, size):
    before, after = (value.shape[:dim], value.shape[dim + 1 :])
    return jnp.moveaxis(value.reshape(*before, size, -1, *after), dim, 0)


def summed_on_arrival(value, axis, dim):
    size = lax.axis_size(axis)
    pieces = lax.all_to_all(in_blocks(value, dim, size), axis, 0, 0, tiled=True)
    return jnp.sum(pieces, axis=0)


def rebalance_rows(points, block_counts, block_dest):
    dp_devices = lax.axis_size(DP)
    dp_index = lax.axis_index(DP)
    nblocks = block_dest.shape[1]
    feature_width = points.shape[1]
    block_rows = points.shape[0] // nblocks
    slot_count = (nblocks + dp_devices - 1) // dp_devices
    blocks = points.reshape(nblocks, block_rows, feature_width)
    my_dest = lax.dynamic_index_in_dim(block_dest, dp_index, 0, keepdims=False)
    my_count = lax.dynamic_index_in_dim(block_counts, dp_index, 0, keepdims=False)
    positions = jnp.arange(nblocks, dtype=jnp.int32)
    targets = jnp.arange(dp_devices, dtype=jnp.int32)
    slot_ids = jnp.arange(slot_count, dtype=jnp.int32)
    send_hits = ((my_dest[:, None] == targets[None, :]) & (positions[:, None] < my_count)).astype(
        jnp.int32
    )
    send_rank = jnp.cumsum(send_hits, axis=0) - send_hits
    chosen = send_hits[:, :, None] * (send_rank[:, :, None] == slot_ids[None, None, :]).astype(
        jnp.int32
    )
    filled = jnp.sum(chosen, axis=0)
    source_block = jnp.sum(chosen * positions[:, None, None], axis=0)
    picked = jnp.take(blocks, source_block.reshape(-1), axis=0).reshape(
        dp_devices, slot_count, block_rows, feature_width
    )
    outgoing = jnp.where(filled[:, :, None, None] > 0, picked, 0.0)
    incoming = lax.all_to_all(outgoing, DP, split_axis=0, concat_axis=0, tiled=True)
    live_all = positions[None, :] < block_counts[:, None]
    sent_here = jnp.sum(((block_dest == dp_index) & live_all).astype(jnp.int32), axis=1)
    full_slot = (slot_ids[None, :] < sent_here[:, None]).astype(jnp.int32).reshape(-1)
    order_rank = jnp.cumsum(full_slot) - full_slot
    pick_slots = jnp.arange(RB, dtype=jnp.int32)
    pick_table = full_slot[None, :] * (order_rank[None, :] == pick_slots[:, None]).astype(jnp.int32)
    pick_index = jnp.sum(
        pick_table * jnp.arange(dp_devices * slot_count, dtype=jnp.int32)[None, :], axis=1
    )
    arrived = jnp.take(
        incoming.reshape(dp_devices * slot_count, block_rows, feature_width), pick_index, axis=0
    )
    return arrived.reshape(RB * block_rows, feature_width)


def densities(points_live, centres, factor_set, weights):
    members = centres.shape[0]
    group_width = math.gcd(members, 8)
    feature_width = centres.shape[1]

    def block_density(inputs):
        centre_set, factor_block, weight_block = inputs
        shifted = points_live[None, :, :] - centre_set[:, None, :]
        projected = jnp.einsum("grd,gde->gre", shifted, factor_block, precision=highest)
        logdet = jnp.sum(jnp.log(jnp.diagonal(factor_block, axis1=1, axis2=2)), axis=1)
        offset_terms = weight_block + logdet - 0.5 * feature_width * log_two_pi
        return offset_terms[:, None] - 0.5 * jnp.sum(projected * projected, axis=2)

    grouped = lax.map(
        block_density,
        (
            centres.reshape(members // group_width, group_width, feature_width),
            factor_set.reshape(members // group_width, group_width, feature_width, feature_width),
            weights.reshape(members // group_width, group_width),
        ),
    )
    return grouped.reshape(members, points_live.shape[0])


def moments(points_live, centres, responsibility):
    members = centres.shape[0]
    group_width = math.gcd(members, 8)
    feature_width = centres.shape[1]

    def block_moments(inputs):
        centre_set, weight_block = inputs
        shifted = points_live[None, :, :] - centre_set[:, None, :]
        weight_sum = jnp.sum(weight_block, axis=1)
        first_moment = jnp.einsum("gr,grd->gd", weight_block, shifted, precision=highest)
        second_moment = jnp.einsum(
            "grd,gre->gde", shifted * weight_block[:, :, None], shifted, precision=highest
        )
        return (weight_sum, first_moment, second_moment)

    weight_sums, firsts, seconds = lax.map(
        block_moments,
        (
            centres.reshape(members // group_width, group_width, feature_width),
            responsibility.reshape(members // group_width, group_width, responsibility.shape[1]),
        ),
    )
    return (
        weight_sums.reshape(members),
        firsts.reshape(members, feature_width),
        seconds.reshape(members, feature_width, feature_width),
    )


def pack_symmetric(matrix):
    half_width = matrix.shape[-1] // 2
    top_left = jnp.triu(matrix[:, :half_width, :half_width]) + jnp.tril(
        matrix[:, half_width:, half_width:], -1
    )
    packed = jnp.concatenate([top_left, matrix[:, :half_width, half_width:]], axis=2)
    corner = jnp.diagonal(matrix[:, half_width:, half_width:], axis1=1, axis2=2)
    return (packed, corner)


def unpack_symmetric(packed, corner):
    half_width = packed.shape[1]
    identity = jnp.eye(half_width, dtype=jnp.float32)
    top_left = packed[:, :, :half_width]
    right_block = packed[:, :, half_width:]
    first_block = jnp.triu(top_left) + jnp.swapaxes(jnp.triu(top_left, 1), 1, 2)
    strict_part = jnp.tril(top_left, -1)
    last_block = strict_part + jnp.swapaxes(strict_part, 1, 2) + corner[:, :, None] * identity
    upper_rows = jnp.concatenate([first_block, right_block], axis=2)
    lower_rows = jnp.concatenate([jnp.swapaxes(right_block, 1, 2), last_block], axis=2)
    return jnp.concatenate([upper_rows, lower_rows], axis=1)


def pack_upper(matrix):
    half_width = matrix.shape[-1] // 2
    top_left = matrix[:, :half_width, :half_width] + jnp.swapaxes(
        jnp.triu(matrix[:, half_width:, half_width:], 1), 1, 2
    )
    packed = jnp.concatenate([top_left, matrix[:, :half_width, half_width:]], axis=2)
    corner = jnp.diagonal(matrix[:, half_width:, half_width:], axis1=1, axis2=2)
    return (packed, corner)


def unpack_upper(packed, corner):
    half_width = packed.shape[1]
    identity = jnp.eye(half_width, dtype=jnp.float32)
    top_left = packed[:, :, :half_width]
    last_block = jnp.swapaxes(jnp.tril(top_left, -1), 1, 2) + corner[:, :, None] * identity
    upper_rows = jnp.concatenate([jnp.triu(top_left), packed[:, :, half_width:]], axis=2)
    lower_rows = jnp.concatenate([jnp.zeros_like(last_block), last_block], axis=2)
    return jnp.concatenate([upper_rows, lower_rows], axis=1)


def gathered_density(points_live, own_params):
    own_centres, own_factors, own_weights = own_params
    members = own_centres.shape[0] * lax.axis_size(DP)
    feature_width = own_centres.shape[1]
    initial = (
        jnp.zeros((members, points_live.shape[0]), jnp.float32),
        jnp.zeros((members, feature_width), jnp.float32),
    )
    packed, corner = pack_upper(own_factors)
    centre_piece = gathered_by_axis(own_centres, DP, (1, 0, 2), 0)
    offset = jnp.int32(0)
    log_table = lax.dynamic_update_slice_in_dim(
        initial[0],
        densities(
            points_live,
            centre_piece,
            unpack_upper(
                gathered_by_axis(packed, DP, (1, 0, 2), 0),
                gathered_by_axis(corner, DP, (1, 0, 2), 0),
            ),
            gathered_by_axis(own_weights, DP, (1, 0, 2), 0),
        ),
        offset,
        0,
    )
    centres = lax.dynamic_update_slice_in_dim(initial[1], centre_piece, offset, 0)
    return (log_table, centres)


def row_responsibility(log_table):
    row_peak = jnp.max(log_table, axis=0)
    row_scaled = jnp.sum(jnp.exp(log_table - row_peak[None, :]), axis=0)

    def combine(earlier, later):
        joint_peak = jnp.maximum(earlier[0], later[0])
        return (
            joint_peak,
            earlier[1] * jnp.exp(earlier[0] - joint_peak)
            + later[1] * jnp.exp(later[0] - joint_peak),
        )

    peak_all, scaled_all = merged((row_peak, row_scaled), "comp", combine)
    log_total = peak_all + jnp.log(scaled_all)
    return (log_total, jnp.exp(log_table - log_total[None, :]))


def summed_moments(statistics):
    weight_sum, first_moment, second_moment = statistics
    packed, corner = pack_symmetric(second_moment)
    totals = (
        summed_on_arrival(weight_sum, DP, 0),
        summed_on_arrival(first_moment, DP, 0),
        summed_on_arrival(packed, DP, 0),
        summed_on_arrival(corner, DP, 0),
    )
    return (totals[0], totals[1], unpack_symmetric(totals[2], totals[3]))


def refresh(centres, weight_sum, first_moment, second_moment, total_points):
    identity = jnp.eye(centres.shape[1], dtype=jnp.float32)
    counted = weight_sum + 1.0
    covariance = (
        second_moment
        - first_moment[:, :, None] * first_moment[:, None, :] / counted[:, None, None]
        + ridge_term * identity
    ) / counted[:, None, None]
    cholesky_lower = jnp.linalg.cholesky(covariance)
    inverse_lower = jax.scipy.linalg.solve_triangular(
        cholesky_lower, jnp.broadcast_to(identity, covariance.shape), lower=True
    )
    return (
        centres + first_moment / counted[:, None],
        jnp.swapaxes(inverse_lower, 1, 2),
        jnp.log(counted / total_points),
    )


def per_device(points, block_counts, block_dest, means, factors, log_weights):
    points_live = rebalance_rows(points, block_counts, block_dest)
    total_points = float(lax.axis_size(DP) * points_live.shape[0] + K)
    current = (means, factors, log_weights)
    for iteration in range(ITERS):
        log_table, centres = gathered_density(points_live, current)
        log_total, responsibility = row_responsibility(log_table)
        weight_sum, first_moment, second_moment = summed_moments(
            moments(points_live, centres, responsibility)
        )
        current = refresh(current[0], weight_sum, first_moment, second_moment, total_points)
    new_means, new_factors, new_weights = current
    return (new_means, new_factors, new_weights, log_total / points.shape[1])


def solution(mesh):
    split = Mesh(
        mesh.devices.reshape(8, 4, 2, mesh.shape["comp"]), ("dp_0", "dp_1", "dp_2", "comp")
    )
    in_specs = (P(DP, None), P(), P(), P(DP_COMP, None), P(DP_COMP, None, None), P(DP_COMP))
    out_specs = (P(DP_COMP, None), P(DP_COMP, None, None), P(DP_COMP), P(DP))
    return jax.shard_map(
        per_device, mesh=split, in_specs=in_specs, out_specs=out_specs, check_vma=False
    )
```

profile of v0, /device:TPU:8, one launch (start us, length us, event | category | flops | bytes accessed | tf_op | source)
XLA Modules:
  0.0 927.8 jit_solution(11059183866429565092)
XLA Ops:
  9.2 13.0 %all-gather.3 = f32[4,64,128]{2,1,0:T(8,128)} all-gather(f32[1,64,128]{2,1,0:T(8,128)S(1)} %copy.268), channel_id=5, replica_groups=mesh['dp_0'=8,'dp_1'=4,'dp_2'=2,'comp'=4] {'dp_1'}, dimensions={0}, use_global_device_ids=true | all-gather | bytes 163840 | tf_op jit(solution)/shard_map/all_gather | solution.py:27
  27.6 12.0 %all-to-all-start = ((f32[64,1,64,128]{3,2,1,0:T(8,128)}), f32[64,1,64,128]{3,2,1,0:T(8,128)}, u32[]{:S(2)}, u32[]{:S(2)}) async-start(f32[64,1,64,128]{3,2,1,0:T(8,128)} %fusion.48), calls=%async_computation | async-start | bytes 4194304 | tf_op jit(solution)/shard_map/all_to_all | solution.py:110
  39.7 34.5 %all-gather.26.cloned.1.call-done = f32[32,64,128]{2,1,0:T(8,128)} async-done(((f32[4,64,128]{2,1,0:T(8,128)}), f32[32,64,128]{2,1,0:T(8,128)}) %all-gather.26.cloned.1.call-update) | async-done | bytes 1048592 | tf_op jit(solution)/shard_map/all_gather | solution.py:27
  78.0 9.6 %all-reduce.11 = (f32[4]{0:T(128)S(1)}, f32[256]{0:T(256)S(1)}) all-reduce(f32[4]{0:T(128)S(1)} %dynamic-update-slice.2, f32[256]{0:T(256)S(1)} %dynamic-update-slice.5), channel_id=2, replica_groups=mesh['dp_0'=8,'dp_1'=4,'dp_2'=2,'comp'=4] {'dp_1'}, use_global_device_ids=true, to_apply=%add.2 | all-reduce | flops 260 | bytes 2080
  88.0 24.3 %all_gather.79 = f32[32,1,64]{2,1,0:T(1,128)S(1)} all-gather(f32[4,1,64]{2,1,0:T(1,128)S(1)} %reshape.913), channel_id=1, replica_groups=mesh['dp_0'=8,'dp_1'=4,'dp_2'=2,'comp'=4] {'dp_0'}, dimensions={0}, use_global_device_ids=true | all-gather | bytes 9216 | tf_op jit(solution)/shard_map/all_gather | solution.py:27
  117.3 14.4 %all-reduce.3 = f32[32]{0:T(128)S(1)} all-reduce(f32[32]{0:T(128)S(1)} %dynamic-update-slice.3), channel_id=3, replica_groups=mesh['dp_0'=8,'dp_1'=4,'dp_2'=2,'comp'=4] {'dp_0'}, use_global_device_ids=true, to_apply=%add.3 | all-reduce | flops 32 | bytes 256
  134.6 8.4 all-gather.17
  143.0 22.2 %all-gather.18 = f32[8,4,128]{2,1,0:T(4,128)S(1)} all-gather(f32[1,4,128]{2,1,0:T(4,128)S(1)} %bitcast.330), channel_id=10, replica_groups=mesh['dp_0'=8,'dp_1'=4,'dp_2'=2,'comp'=4] {'dp_0'}, dimensions={0}, use_global_device_ids=true | all-gather | bytes 18432 | tf_op jit(solution)/shard_map/all_gather | solution.py:27
  186.9 7.4 copy.337
  196.5 92.3 %while.52 = (s32[]{:T(128)}, f32[8,8,256]{2,1,0:T(8,128)S(1)}, f32[8,8]{1,0:T(8,128)S(1)}, f32[8,8,128,128]{2,3,1,0:T(8,128)}, f32[4,64,128]{2,1,0:T(8,128)S(1)}, /*index=5*/f32[8,8,128]{2,1,0:T(8,128)S(1)}, s32[]{:T(128)}) while((s32[]{:T(128)}, f32[8,8,256]{2,1,0:T(8,128)S(1)}, f32[8,8]{1,0:T(8,128)S(1)}, f32[8,8,128,128]{2,3,1,0:T(8,128)}, ...), condition=%wide.region_9.10_spmd, body=%wide.region_6.9_spmd.sunk | while | flops 403443200 | bytes 2803933 | solution.py:139
  198.8 7.4 copy.392
  210.3 7.4 copy.392
  221.8 7.4 copy.392
  233.4 7.4 copy.392
  244.9 7.4 copy.392
  256.4 7.4 copy.392
  268.0 7.4 copy.392
  279.5 7.4 copy.392
  302.6 31.7 %while.53 = (s32[]{:T(128)}, f32[8,8]{1,0:T(8,128)S(1)}, f32[8,8,128]{2,1,0:T(8,128)}, f32[8,8,128,128]{3,2,1,0:T(8,128)}, f32[8,8,256]{2,1,0:T(8,128)S(1)}, /*i...) while((s32[]{:T(128)}, f32[8,8]{1,0:T(8,128)S(1)}, ...), condition=%wide.region_14.15_spmd, body=%wide.region_12.14_spmd.sunk | while | flops 406849536 | bytes 1254601 | solution.py:165
  354.2 10.3 %all-to-all-start.5 = ((f32[64,1,64]{2,1,0:T(1,128)}), f32[64,1,64]{2,1,0:T(1,128)S(1)}, u32[]{:S(2)}, u32[]{:S(2)}) async-start(f32[64,1,64]{2,1,0:T(1,128)} %copy.297), calls=%async_computation.5 | async-start | bytes 65536 | tf_op jit(solution)/shard_map/all_to_all | solution.py:80
  373.1 9.3 %all-to-all-start.2 = ((f32[64,1,128]{2,1,0:T(1,128)}), f32[64,1,128]{2,1,0:T(1,128)S(1)}, u32[]{:S(2)}, u32[]{:S(2)}) async-start(f32[64,1,128]{2,1,0:T(1,128)} %bitcast.68), calls=%async_computation.2 | async-start | bytes 65536 | tf_op jit(solution)/shard_map/all_to_all | solution.py:80
  391.0 9.9 %all-to-all-start.4 = ((f32[64,1,64,128]{3,2,1,0:T(8,128)}), f32[64,1,64,128]{3,2,1,0:T(8,128)S(1)}, u32[]{:S(2)}, u32[]{:S(2)}) async-start(f32[64,1,64,128]{3,2,1,0:T(8,128)} %copy.291), calls=%async_computation.4 | async-start | bytes 4194304 | tf_op jit(solution)/shard_map/all_to_all | solution.py:80
  402.9 49.3 %all-to-all-done.4 = f32[64,1,64,128]{3,2,1,0:T(8,128)S(1)} async-done(((f32[64,1,64,128]{3,2,1,0:T(8,128)}), f32[64,1,64,128]{3,2,1,0:T(8,128)S(1)}, u32[]{:S(2)}, u32[]{:S(2)}) %all-to-all-start.4) | async-done | bytes 2097184 | tf_op jit(solution)/shard_map/all_to_all | solution.py:80
  452.9 11.7 %custom-call.20 = f32[1,128,128]{2,1,0:T(8,128)S(1)} custom-call(f32[1,128,128]{2,1,0:T(8,128)S(1)} %fusion.54), custom_call_target="Cholesky" | custom-call | tf_op jit(solution)/shard_map/jit(cholesky)/cholesky | solution.py:288
  466.0 9.8 %custom-call.21 = f32[1,128,128]{1,2,0:T(8,128)S(1)} custom-call(f32[1,128,128]{2,1,0:T(8,128)S(1)} %select_select_fusion.1), custom_call_target="InvertDiagBlocksLowerTriangular" | custom-call | tf_op jit(solution)/shard_map/jit(_solve_triangular)/triangular_solve | solution.py:289
  476.4 12.8 %all-gather.10 = f32[4,64,128]{2,1,0:T(8,128)} all-gather(f32[1,64,128]{2,1,0:T(8,128)S(1)} %copy.302), channel_id=12, replica_groups=mesh['dp_0'=8,'dp_1'=4,'dp_2'=2,'comp'=4] {'dp_1'}, dimensions={0}, use_global_device_ids=true | all-gather | bytes 163840 | tf_op jit(solution)/shard_map/all_gather | solution.py:27
  489.3 32.6 %all-gather.30.cloned.1.call-done = f32[32,64,128]{2,1,0:T(8,128)} async-done(((f32[4,64,128]{2,1,0:T(8,128)}), f32[32,64,128]{2,1,0:T(8,128)}) %all-gather.30.cloned.1.call-update) | async-done | bytes 1048592 | tf_op jit(solution)/shard_map/all_gather | solution.py:27
  522.7 7.8 all-gather.19
  530.5 21.2 %all-gather.20 = f32[8,4,128]{2,1,0:T(4,128)S(1)} all-gather(f32[1,4,128]{2,1,0:T(4,128)S(1)} %bitcast.331), channel_id=17, replica_groups=mesh['dp_0'=8,'dp_1'=4,'dp_2'=2,'comp'=4] {'dp_0'}, dimensions={0}, use_global_device_ids=true | all-gather | bytes 18432 | tf_op jit(solution)/shard_map/all_gather | solution.py:27
  554.6 10.1 %all-reduce.10 = (f32[4]{0:T(128)S(1)}, f32[256]{0:T(256)S(1)}) all-reduce(f32[4]{0:T(128)S(1)} %dynamic-update-slice.6, f32[256]{0:T(256)S(1)} %dynamic-update-slice.9), channel_id=1, replica_groups=mesh['dp_0'=8,'dp_1'=4,'dp_2'=2,'comp'=4] {'dp_1'}, use_global_device_ids=true, to_apply=%add.6 | all-reduce | flops 260 | bytes 2080
  564.9 21.5 %all_gather.91 = f32[32,1,64]{2,1,0:T(1,128)S(1)} all-gather(f32[4,1,64]{2,1,0:T(1,128)S(1)} %reshape.920), channel_id=1, replica_groups=mesh['dp_0'=8,'dp_1'=4,'dp_2'=2,'comp'=4] {'dp_0'}, dimensions={0}, use_global_device_ids=true | all-gather | bytes 9216 | tf_op jit(solution)/shard_map/all_gather | solution.py:27
  588.5 15.4 %all-reduce.7 = f32[32]{0:T(128)S(1)} all-reduce(f32[32]{0:T(128)S(1)} %dynamic-update-slice.7), channel_id=1, replica_groups=mesh['dp_0'=8,'dp_1'=4,'dp_2'=2,'comp'=4] {'dp_0'}, use_global_device_ids=true, to_apply=%add.7 | all-reduce | flops 32 | bytes 256
  638.8 92.3 %while.54 = (s32[]{:T(128)}, f32[8,8,256]{2,1,0:T(8,128)S(1)}, f32[8,8]{1,0:T(8,128)S(1)}, f32[8,8,128,128]{2,3,1,0:T(8,128)}, f32[4,64,128]{2,1,0:T(8,128)S(1)}, /*index=5*/f32[8,8,128]{2,1,0:T(8,128)S(1)}, s32[]{:T(128)}) while((s32[]{:T(128)}, f32[8,8,256]{2,1,0:T(8,128)S(1)}, f32[8,8]{1,0:T(8,128)S(1)}, f32[8,8,128,128]{2,3,1,0:T(8,128)}, ...), condition=%wide.region_24.27_spmd, body=%wide.region_21.26_spmd.sunk | while | flops 403443200 | bytes 2803933 | solution.py:139
  641.1 7.4 copy.395
  652.6 7.4 copy.395
  664.1 7.4 copy.395
  675.7 7.4 copy.395
  687.2 7.4 copy.395
  698.7 7.4 copy.395
  710.3 7.4 copy.395
  721.8 7.4 copy.395
  745.4 31.7 %while.55 = (s32[]{:T(128)}, f32[8,8]{1,0:T(8,128)S(1)}, f32[8,8,128]{2,1,0:T(8,128)}, f32[8,8,128,128]{3,2,1,0:T(8,128)}, f32[8,8,256]{2,1,0:T(8,128)S(1)}, /*i...) while((s32[]{:T(128)}, f32[8,8]{1,0:T(8,128)S(1)}, ...), condition=%wide.region_29.32_spmd, body=%wide.region_27.31_spmd.sunk | while | flops 406849536 | bytes 1254601 | solution.py:165
  797.0 10.3 %all-to-all-start.10 = ((f32[64,1,64]{2,1,0:T(1,128)}), f32[64,1,64]{2,1,0:T(1,128)S(1)}, u32[]{:S(2)}, u32[]{:S(2)}) async-start(f32[64,1,64]{2,1,0:T(1,128)} %copy.327), calls=%async_computation.10 | async-start | bytes 65536 | tf_op jit(solution)/shard_map/all_to_all | solution.py:80
  815.9 9.3 %all-to-all-start.7 = ((f32[64,1,128]{2,1,0:T(1,128)}), f32[64,1,128]{2,1,0:T(1,128)S(1)}, u32[]{:S(2)}, u32[]{:S(2)}) async-start(f32[64,1,128]{2,1,0:T(1,128)} %bitcast.109), calls=%async_computation.7 | async-start | bytes 65536 | tf_op jit(solution)/shard_map/all_to_all | solution.py:80
  833.8 10.3 %all-to-all-start.9 = ((f32[64,1,64,128]{3,2,1,0:T(8,128)}), f32[64,1,64,128]{3,2,1,0:T(8,128)S(1)}, u32[]{:S(2)}, u32[]{:S(2)}) async-start(f32[64,1,64,128]{3,2,1,0:T(8,128)} %copy.321), calls=%async_computation.9 | async-start | bytes 4194304 | tf_op jit(solution)/shard_map/all_to_all | solution.py:80
  846.2 49.0 %all-to-all-done.9 = f32[64,1,64,128]{3,2,1,0:T(8,128)S(1)} async-done(((f32[64,1,64,128]{3,2,1,0:T(8,128)}), f32[64,1,64,128]{3,2,1,0:T(8,128)S(1)}, u32[]{:S(2)}, u32[]{:S(2)}) %all-to-all-start.9) | async-done | bytes 2097184 | tf_op jit(solution)/shard_map/all_to_all | solution.py:80
  896.0 11.7 %custom-call.22 = f32[1,128,128]{2,1,0:T(8,128)S(1)} custom-call(f32[1,128,128]{2,1,0:T(8,128)S(1)} %fusion.52), custom_call_target="Cholesky" | custom-call | tf_op jit(solution)/shard_map/jit(cholesky)/cholesky | solution.py:288
  909.0 9.8 %custom-call.23 = f32[1,128,128]{1,2,0:T(8,128)S(1)} custom-call(f32[1,128,128]{2,1,0:T(8,128)S(1)} %select_select_fusion), custom_call_target="InvertDiagBlocksLowerTriangular" | custom-call | tf_op jit(solution)/shard_map/jit(_solve_triangular)/triangular_solve | solution.py:289
  (476 shorter events, 320.9 us)
Async XLA Ops:
  7.2 18.1 %copy-start = (f32[1024,128]{1,0:T(8,128)S(1)}, f32[1024,128]{1,0:T(8,128)}, u32[]{:S(2)}) copy-start(f32[1024,128]{1,0:T(8,128)} %param.17) | copy-start | bytes 1572868
  7.2 67.0 %all-gather.26.cloned.1.call-start = ((), (), s32[]{:S(2)}) async-start(), calls=%async_computation.11 | async-start | bytes 1179648 | tf_op jit(solution)/shard_map/all_gather | solution.py:27
  27.6 47.3 %copy-start.10 = (u32[256]{0:T(256)S(1)}, u32[256]{0:T(256)}, u32[]{:S(2)}) copy-start(u32[256]{0:T(256)} %constant.370) | copy-start | bytes 3076
  27.6 59.9 %copy-start.5 = (s32[64,16]{0,1:T(8,128)S(1)}, s32[64,16]{0,1:T(8,128)}, u32[]{:S(2)}) copy-start(s32[64,16]{0,1:T(8,128)} %param.19) | copy-start | bytes 12292
  27.6 59.9 %copy-start.7 = (s32[64]{0:T(128)S(1)}, s32[64]{0:T(128)}, u32[]{:S(2)}) copy-start(s32[64]{0:T(128)} %param.18) | copy-start | bytes 772
  27.6 86.8 %copy-start.9 = (u32[256]{0:T(256)S(1)}, u32[256]{0:T(256)}, u32[]{:S(2)}) copy-start(u32[256]{0:T(256)} %constant.375) | copy-start | bytes 3076
  27.6 87.4 %copy-start.8 = (u32[256]{0:T(256)S(1)}, u32[256]{0:T(256)}, u32[]{:S(2)}) copy-start(u32[256]{0:T(256)} %constant.380) | copy-start | bytes 3076
  27.6 107.0 %copy-start.6 = (f32[1,128]{1,0:T(1,128)S(1)}, f32[1,128]{1,0:T(1,128)}, u32[]{:S(2)}) copy-start(f32[1,128]{1,0:T(1,128)} %param.20) | copy-start | bytes 1540
  27.6 166.7 %all-to-all-start = ((f32[64,1,64,128]{3,2,1,0:T(8,128)}), f32[64,1,64,128]{3,2,1,0:T(8,128)}, u32[]{:S(2)}, u32[]{:S(2)}) async-start(f32[64,1,64,128]{3,2,1,0:T(8,128)} %fusion.48), calls=%async_computation | async-start | bytes 4194304 | tf_op jit(solution)/shard_map/all_to_all | solution.py:110
  39.7 127.8 %all-gather.28.cloned.1.call-start = ((), (), s32[]{:S(2)}) async-start(), calls=%async_computation.12 | async-start | bytes 3145728 | tf_op jit(solution)/shard_map/all_gather | solution.py:27
  289.5 9.8 %all-to-all-start.1 = ((f32[4,2,256]{2,1,0:T(2,128)}), f32[4,2,256]{2,1,0:T(2,128)S(1)}, u32[]{:S(2)}, u32[]{:S(2)}) async-start(f32[4,2,256]{2,1,0:T(2,128)} %broadcast_in_dim.229), calls=%async_computation.1 | async-start | bytes 16384 | tf_op jit(solution)/shard_map/all_to_all | solution.py:40
  335.0 19.2 %all-to-all-start.3 = ((f32[64,1,1]{2,1,0:T(1,128)}), f32[64,1,1]{2,1,0:T(1,128)S(1)}, u32[]{:S(2)}, u32[]{:S(2)}) async-start(f32[64,1,1]{2,1,0:T(1,128)} %all_to_all.52), calls=%async_computation.3 | async-start | bytes 65536 | tf_op jit(solution)/shard_map/all_to_all | solution.py:80
  354.2 18.9 %all-to-all-start.5 = ((f32[64,1,64]{2,1,0:T(1,128)}), f32[64,1,64]{2,1,0:T(1,128)S(1)}, u32[]{:S(2)}, u32[]{:S(2)}) async-start(f32[64,1,64]{2,1,0:T(1,128)} %copy.297), calls=%async_computation.5 | async-start | bytes 65536 | tf_op jit(solution)/shard_map/all_to_all | solution.py:80
  368.7 13.8 %copy-start.4 = (f32[64,64,64]{0,2,1:T(8,128)S(1)}, f32[64,64,64]{0,2,1:T(8,128)}, u32[]{:S(2)}) copy-start(f32[64,64,64]{0,2,1:T(8,128)} %select_add_fusion.1) | copy-start | bytes 3145732
  373.1 17.9 %all-to-all-start.2 = ((f32[64,1,128]{2,1,0:T(1,128)}), f32[64,1,128]{2,1,0:T(1,128)S(1)}, u32[]{:S(2)}, u32[]{:S(2)}) async-start(f32[64,1,128]{2,1,0:T(1,128)} %bitcast.68), calls=%async_computation.2 | async-start | bytes 65536 | tf_op jit(solution)/shard_map/all_to_all | solution.py:80
  391.0 61.1 %all-to-all-start.4 = ((f32[64,1,64,128]{3,2,1,0:T(8,128)}), f32[64,1,64,128]{3,2,1,0:T(8,128)S(1)}, u32[]{:S(2)}, u32[]{:S(2)}) async-start(f32[64,1,64,128]{3,2,1,0:T(8,128)} %copy.291), calls=%async_computation.4 | async-start | bytes 4194304 | tf_op jit(solution)/shard_map/all_to_all | solution.py:80
  400.9 120.9 %all-gather.30.cloned.1.call-start = ((), (), s32[]{:S(2)}) async-start(), calls=%async_computation.13 | async-start | bytes 1179648 | tf_op jit(solution)/shard_map/all_gather | solution.py:27
  489.2 117.8 %all-gather.32.cloned.1.call-start = ((), (), s32[]{:S(2)}) async-start(), calls=%async_computation.14 | async-start | bytes 3145728 | tf_op jit(solution)/shard_map/all_gather | solution.py:27
  622.3 3.4 copy-start.2
  731.8 9.8 %all-to-all-start.6 = ((f32[4,2,256]{2,1,0:T(2,128)}), f32[4,2,256]{2,1,0:T(2,128)S(1)}, u32[]{:S(2)}, u32[]{:S(2)}) async-start(f32[4,2,256]{2,1,0:T(2,128)} %broadcast_in_dim.234), calls=%async_computation.6 | async-start | bytes 16384 | tf_op jit(solution)/shard_map/all_to_all | solution.py:40
  777.8 19.2 %all-to-all-start.8 = ((f32[64,1,1]{2,1,0:T(1,128)}), f32[64,1,1]{2,1,0:T(1,128)S(1)}, u32[]{:S(2)}, u32[]{:S(2)}) async-start(f32[64,1,1]{2,1,0:T(1,128)} %all_to_all.53), calls=%async_computation.8 | async-start | bytes 65536 | tf_op jit(solution)/shard_map/all_to_all | solution.py:80
  797.0 18.9 %all-to-all-start.10 = ((f32[64,1,64]{2,1,0:T(1,128)}), f32[64,1,64]{2,1,0:T(1,128)S(1)}, u32[]{:S(2)}, u32[]{:S(2)}) async-start(f32[64,1,64]{2,1,0:T(1,128)} %copy.327), calls=%async_computation.10 | async-start | bytes 65536 | tf_op jit(solution)/shard_map/all_to_all | solution.py:80
  811.5 13.8 %copy-start.3 = (f32[64,64,64]{0,2,1:T(8,128)S(1)}, f32[64,64,64]{0,2,1:T(8,128)}, u32[]{:S(2)}) copy-start(f32[64,64,64]{0,2,1:T(8,128)} %select_add_fusion) | copy-start | bytes 3145732
  815.9 17.9 %all-to-all-start.7 = ((f32[64,1,128]{2,1,0:T(1,128)}), f32[64,1,128]{2,1,0:T(1,128)S(1)}, u32[]{:S(2)}, u32[]{:S(2)}) async-start(f32[64,1,128]{2,1,0:T(1,128)} %bitcast.109), calls=%async_computation.7 | async-start | bytes 65536 | tf_op jit(solution)/shard_map/all_to_all | solution.py:80
  833.8 61.4 %all-to-all-start.9 = ((f32[64,1,64,128]{3,2,1,0:T(8,128)}), f32[64,1,64,128]{3,2,1,0:T(8,128)S(1)}, u32[]{:S(2)}, u32[]{:S(2)}) async-start(f32[64,1,64,128]{3,2,1,0:T(8,128)} %copy.321), calls=%async_computation.9 | async-start | bytes 4194304 | tf_op jit(solution)/shard_map/all_to_all | solution.py:80
  844.1 75.8 %copy-start.1 = (f32[1024,128]{1,0:T(8,128)S(1)}, f32[1024,128]{1,0:T(8,128)}, u32[]{:S(2)}) copy-start(f32[1024,128]{1,0:T(8,128)} %param.17) | copy-start | bytes 1572868
Sparse Core Ops, SparseCore 0:
  22.3 51.8 all-gather.25
  76.0 15.5 all-gather.27
  489.3 32.4 all-gather.29
  523.5 14.2 all-gather.31
where the time goes:
time: 934 us; the launch traced here: 928 us
  local copies, waits for them, and re-layouts  279 us (30%)
  blocking collectives  193 us (21%)
  waiting for transfers between devices  179 us (19%)
  starting transfers between devices  94.7 us (10%)
  other arithmetic  93.8 us (10%)
  matrix products  68 us (7%)
  between operations  19.9 us (2%)
    all_gather x12, blocking collectives, stacked_from(): pieces = lax.all_gather(pieces, axes[k], axis=0, tiled=True)  139 us
    squeeze x32, local copies, waits for them, and re-layouts, densities(): lax.map(block_density, (centres.reshape(members // group_width, group_wid...  135 us
    all_to_all x8, waiting for transfers between devices, summed_on_arrival(): pieces = lax.all_to_all(in_blocks(value, dim, size), axis, 0, 0, tiled=True)  101 us
    all_to_all x8, starting transfers between devices, summed_on_arrival(): pieces = lax.all_to_all(in_blocks(value, dim, size), axis, 0, 0, tiled=True)  73.2 us
    all_gather x4, waiting for transfers between devices, stacked_from(): pieces = lax.all_gather(pieces, axes[k], axis=0, tiled=True)  67.1 us
    unnamed x6, blocking collectives  54.6 us
    unnamed x59, local copies, waits for them, and re-layouts  35.6 us
    dot_general x16, matrix products, block_moments(): jnp.einsum('grd,gre->gde', shifted * weight_block[:, :, None], shifted, p...  33.4 us
  transfers between devices with their start and end apart: 15, of which 10 were waited for; matrix products, arithmetic and copies ran while one was open for 11% of the time, Pallas kernels for 0%

commit v1 on v0

--- a/solution.py
+++ b/solution.py
@@ -24,7 +24,10 @@
 def stacked_from(value, axes, sequence):
     pieces = value[None]
     for k in sequence:
-        pieces = lax.all_gather(pieces, axes[k], axis=0, tiled=True)
+        count = lax.axis_size(axes[k])
+        parts = jnp.stack([pieces for _ in range(count)])
+        parts = lax.all_to_all(parts, axes[k], split_axis=0, concat_axis=0)
+        pieces = jnp.concatenate(parts, axis=0)
     block = [lax.axis_size(axes[k]) for k in reversed(sequence)]
     pieces = pieces.reshape(*block, *value.shape)
     turned = sorted(range(len(sequence)), key=lambda place: sequence[len(sequence) - 1 - place])

time: 934 us -> 900 us (0.964)
  blocking collectives: 193 us -> 65.1 us
  waiting for transfers between devices: 179 us -> 231 us
  starting transfers between devices: 94.7 us -> 139 us
  between operations: 19.9 us -> 4.91 us
  other arithmetic: 93.8 us -> 104 us
    all_gather x12 -> x0, blocking collectives: 139 us -> none  [stacked_from(): pieces = lax.all_gather(pieces, axes[k], axis=0, tiled=True)]
    all_to_all x0 -> x15, waiting for transfers between devices: none -> 88.9 us  [stacked_from(): parts = lax.all_to_all(parts, axes[k], split_axis=0, concat_axis=0)]
    all_gather x4 -> x0, waiting for transfers between devices: 67.1 us -> none  [stacked_from(): pieces = lax.all_gather(pieces, axes[k], axis=0, tiled=True)]
    all_to_all x0 -> x15, starting transfers between devices: none -> 66.5 us  [stacked_from(): parts = lax.all_to_all(parts, axes[k], split_axis=0, concat_axis=0)]
    all_to_all x0 -> x10, blocking collectives: none -> 65.1 us  [the longest x9 51.3 us: stacked_from(): parts = lax.all_to_all(parts, axes[k], split_axis=0, concat_axis=0)]
    unnamed x6 -> x0, blocking collectives: 54.6 us -> none
    all_to_all x1, waiting for transfers between devices: 0.01 us -> 23.2 us  [rebalance_rows(): lax.all_to_all(outgoing, DP, split_axis=0, concat_axis=0, tiled=True)]
    all_to_all x8 -> x7, starting transfers between devices: 73.2 us -> 57.4 us  [summed_on_arrival(): pieces = lax.all_to_all(in_blocks(value, dim, size), axis, 0, 0, tiled=True)]
  transfers between devices with their start and end apart: 15 -> 25, of which waited for: 10 -> 20; matrix products, arithmetic and copies ran while one was open for 11% -> 12% of each run, Pallas kernels for 0% -> 0%
where the time goes in v1:
time: 900 us; the launch traced here: 892 us
  local copies, waits for them, and re-layouts  280 us (31%)
  waiting for transfers between devices  231 us (26%)
  starting transfers between devices  139 us (15%)
  other arithmetic  104 us (12%)
  matrix products  68 us (8%)
  blocking collectives  65.1 us (7%)
    squeeze x32, local copies, waits for them, and re-layouts, densities(): lax.map(block_density, (centres.reshape(members // group_width, group_wid...  135 us
    all_to_all x7, waiting for transfers between devices, summed_on_arrival(): pieces = lax.all_to_all(in_blocks(value, dim, size), axis, 0, 0, tiled=True)  109 us
    all_to_all x15, waiting for transfers between devices, stacked_from(): parts = lax.all_to_all(parts, axes[k], split_axis=0, concat_axis=0)  88.9 us
    all_to_all x15, starting transfers between devices, stacked_from(): parts = lax.all_to_all(parts, axes[k], split_axis=0, concat_axis=0)  66.5 us
    all_to_all x7, starting transfers between devices, summed_on_arrival(): pieces = lax.all_to_all(in_blocks(value, dim, size), axis, 0, 0, tiled=True)  57.4 us
    all_to_all x9, blocking collectives, stacked_from(): parts = lax.all_to_all(parts, axes[k], split_axis=0, concat_axis=0)  51.3 us
    dot_general x16, matrix products, block_moments(): jnp.einsum('grd,gre->gde', shifted * weight_block[:, :, None], shifted, p...  33.3 us
    unnamed x44, local copies, waits for them, and re-layouts  32.7 us
  transfers between devices with their start and end apart: 25, of which 20 were waited for; matrix products, arithmetic and copies ran while one was open for 12% of the time, Pallas kernels for 0%

profile of v1, /device:TPU:8, one launch (start us, length us, event | category | flops | bytes accessed | tf_op | source)
XLA Modules:
  0.0 892.5 jit_solution(5718596401190499203)
XLA Ops:
  11.8 8.0 all-to-all-start.1
  20.6 6.8 all-to-all-done.1
  50.4 6.7 all-to-all-done.7
  61.2 7.6 all-to-all-done.11
  68.8 8.2 all_to_all.185
  89.6 13.7 %all-to-all-done.4 = f32[8,4,1,64,128]{4,3,1,2,0:T(8,128)} async-done(((f32[8,4,1,64,128]{4,3,1,2,0:T(8,128)}), f32[8,4,1,64,128]{4,3,1,2,0:T(8,128)}, u32[]{:S(2)}, u32[]{:S(2)}) %all-to-all-start.4) | async-done | bytes 1048608 | tf_op jit(solution)/shard_map/all_to_all | solution.py:29
  117.1 6.6 all_to_all.188
  123.7 6.7 all-to-all-start.9
  150.9 7.4 copy.329
  158.3 23.2 %all-to-all-done.9 = f32[64,1,64,128]{3,2,1,0:T(8,128)} async-done(((f32[64,1,64,128]{3,2,1,0:T(8,128)}), f32[64,1,64,128]{3,2,1,0:T(8,128)}, u32[]{:S(2)}, u32[]{:S(2)}) %all-to-all-start.9) | async-done | bytes 2097184 | tf_op jit(solution)/shard_map/all_to_all | solution.py:113
  183.8 92.3 %while.52 = (s32[]{:T(128)}, f32[8,8,256]{2,1,0:T(8,128)S(1)}, f32[8,8]{1,0:T(8,128)S(1)}, f32[8,8,128,128]{2,3,1,0:T(8,128)}, f32[4,64,128]{2,1,0:T(8,128)S(1)}, /*index=5*/f32[8,8,128]{2,1,0:T(8,128)S(1)}, s32[]{:T(128)}) while((s32[]{:T(128)}, f32[8,8,256]{2,1,0:T(8,128)S(1)}, f32[8,8]{1,0:T(8,128)S(1)}, f32[8,8,128,128]{2,3,1,0:T(8,128)}, ...), condition=%wide.region_9.10_spmd, body=%wide.region_6.9_spmd.sunk | while | flops 403443200 | bytes 2803933 | solution.py:142
  186.0 7.4 copy.384
  197.5 7.4 copy.384
  209.1 7.4 copy.384
  220.6 7.4 copy.384
  232.2 7.4 copy.384
  243.7 7.4 copy.384
  255.2 7.4 copy.384
  266.8 7.4 copy.384
  289.8 31.7 %while.53 = (s32[]{:T(128)}, f32[8,8]{1,0:T(8,128)S(1)}, f32[8,8,128]{2,1,0:T(8,128)}, f32[8,8,128,128]{3,2,1,0:T(8,128)}, f32[8,8,256]{2,1,0:T(8,128)S(1)}, /*i...) while((s32[]{:T(128)}, f32[8,8]{1,0:T(8,128)S(1)}, ...), condition=%wide.region_14.15_spmd, body=%wide.region_12.14_spmd.sunk | while | flops 406849536 | bytes 1254601 | solution.py:168
  321.6 13.9 %all_to_all.194 = f32[64,1,1]{2,1,0:T(1,128)S(1)} all-to-all(f32[64,1,1]{2,1,0:T(1,128)S(1)} %all_to_all.148), channel_id=1, replica_groups=mesh['dp_0'=8,'dp_1'=4,'dp_2'=2,'comp'=4] {'dp_0','dp_1','dp_2'}, dimensions={0} | all-to-all | bytes 512 | tf_op jit(solution)/shard_map/all_to_all | solution.py:83
  336.9 7.6 all_to_all.189
  361.5 6.9 all-to-all-start.17
  381.5 8.5 all-to-all-done.20
  415.1 11.2 %all-to-all-start.19 = ((f32[64,1,64,128]{3,2,1,0:T(8,128)}), f32[64,1,64,128]{3,2,1,0:T(8,128)S(1)}, u32[]{:S(2)}, u32[]{:S(2)}) async-start(f32[64,1,64,128]{3,2,1,0:T(8,128)} %copy.284), calls=%async_computation.19 | async-start | bytes 4194304 | tf_op jit(solution)/shard_map/all_to_all | solution.py:83
  427.6 49.7 %all-to-all-done.19 = f32[64,1,64,128]{3,2,1,0:T(8,128)S(1)} async-done(((f32[64,1,64,128]{3,2,1,0:T(8,128)}), f32[64,1,64,128]{3,2,1,0:T(8,128)S(1)}, u32[]{:S(2)}, u32[]{:S(2)}) %all-to-all-start.19) | async-done | bytes 2097184 | tf_op jit(solution)/shard_map/all_to_all | solution.py:83
  478.1 11.7 %custom-call.20 = f32[1,128,128]{2,1,0:T(8,128)S(1)} custom-call(f32[1,128,128]{2,1,0:T(8,128)S(1)} %fusion.54), custom_call_target="Cholesky" | custom-call | tf_op jit(solution)/shard_map/jit(cholesky)/cholesky | solution.py:291
  491.2 9.8 %custom-call.21 = f32[1,128,128]{1,2,0:T(8,128)S(1)} custom-call(f32[1,128,128]{2,1,0:T(8,128)S(1)} %select_select_fusion.1), custom_call_target="InvertDiagBlocksLowerTriangular" | custom-call | tf_op jit(solution)/shard_map/jit(_solve_triangular)/triangular_solve | solution.py:292
  515.5 7.6 all-to-all-done.25
  535.0 8.4 all_to_all.192
  549.8 26.5 %all-to-all-done.22 = f32[8,4,1,64,128]{4,3,1,2,0:T(8,128)S(1)} async-done(((f32[8,4,1,64,128]{4,3,1,2,0:T(8,128)}), f32[8,4,1,64,128]{4,3,1,2,0:T(8,128)S(1)}, u32[]{:S(2)}, u32[]{:S(2)}) %all-to-all-start.22) | async-done | bytes 1048608 | tf_op jit(solution)/shard_map/all_to_all | solution.py:29
  605.1 7.4 copy.330
  612.4 92.3 %while.54 = (s32[]{:T(128)}, f32[8,8,256]{2,1,0:T(8,128)S(1)}, f32[8,8]{1,0:T(8,128)S(1)}, f32[8,8,128,128]{2,3,1,0:T(8,128)}, f32[4,64,128]{2,1,0:T(8,128)S(1)}, /*index=5*/f32[8,8,128]{2,1,0:T(8,128)S(1)}, s32[]{:T(128)}) while((s32[]{:T(128)}, f32[8,8,256]{2,1,0:T(8,128)S(1)}, f32[8,8]{1,0:T(8,128)S(1)}, f32[8,8,128,128]{2,3,1,0:T(8,128)}, ...), condition=%wide.region_24.27_spmd, body=%wide.region_21.26_spmd.sunk | while | flops 403443200 | bytes 2803933 | solution.py:142
  614.7 7.4 copy.387
  626.2 7.4 copy.387
  637.7 7.4 copy.387
  649.3 7.4 copy.387
  660.8 7.4 copy.387
  672.3 7.4 copy.387
  683.9 7.4 copy.387
  695.4 7.4 copy.387
  718.0 31.7 %while.55 = (s32[]{:T(128)}, f32[8,8]{1,0:T(8,128)S(1)}, f32[8,8,128]{2,1,0:T(8,128)}, f32[8,8,128,128]{3,2,1,0:T(8,128)}, f32[8,8,256]{2,1,0:T(8,128)S(1)}, /*i...) while((s32[]{:T(128)}, f32[8,8]{1,0:T(8,128)S(1)}, ...), condition=%wide.region_29.32_spmd, body=%wide.region_27.31_spmd.sunk | while | flops 406849536 | bytes 1254601 | solution.py:168
  768.1 10.4 %all-to-all-start.34 = ((f32[64,1,64]{2,1,0:T(1,128)}), f32[64,1,64]{2,1,0:T(1,128)S(1)}, u32[]{:S(2)}, u32[]{:S(2)}) async-start(f32[64,1,64]{2,1,0:T(1,128)} %copy.319), calls=%async_computation.34 | async-start | bytes 65536 | tf_op jit(solution)/shard_map/all_to_all | solution.py:83
  787.1 9.4 %all-to-all-start.31 = ((f32[64,1,128]{2,1,0:T(1,128)}), f32[64,1,128]{2,1,0:T(1,128)S(1)}, u32[]{:S(2)}, u32[]{:S(2)}) async-start(f32[64,1,128]{2,1,0:T(1,128)} %bitcast.115), calls=%async_computation.31 | async-start | bytes 65536 | tf_op jit(solution)/shard_map/all_to_all | solution.py:83
  805.1 10.3 %all-to-all-start.33 = ((f32[64,1,64,128]{3,2,1,0:T(8,128)}), f32[64,1,64,128]{3,2,1,0:T(8,128)S(1)}, u32[]{:S(2)}, u32[]{:S(2)}) async-start(f32[64,1,64,128]{3,2,1,0:T(8,128)} %copy.313), calls=%async_computation.33 | async-start | bytes 4194304 | tf_op jit(solution)/shard_map/all_to_all | solution.py:83
  817.4 49.0 %all-to-all-done.33 = f32[64,1,64,128]{3,2,1,0:T(8,128)S(1)} async-done(((f32[64,1,64,128]{3,2,1,0:T(8,128)}), f32[64,1,64,128]{3,2,1,0:T(8,128)S(1)}, u32[]{:S(2)}, u32[]{:S(2)}) %all-to-all-start.33) | async-done | bytes 2097184 | tf_op jit(solution)/shard_map/all_to_all | solution.py:83
  867.2 11.7 %custom-call.22 = f32[1,128,128]{2,1,0:T(8,128)S(1)} custom-call(f32[1,128,128]{2,1,0:T(8,128)S(1)} %fusion.52), custom_call_target="Cholesky" | custom-call | tf_op jit(solution)/shard_map/jit(cholesky)/cholesky | solution.py:291
  880.3 9.8 %custom-call.23 = f32[1,128,128]{1,2,0:T(8,128)S(1)} custom-call(f32[1,128,128]{2,1,0:T(8,128)S(1)} %select_select_fusion), custom_call_target="InvertDiagBlocksLowerTriangular" | custom-call | tf_op jit(solution)/shard_map/jit(_solve_triangular)/triangular_solve | solution.py:292
  (503 shorter events, 403.8 us)
Async XLA Ops:
  0.6 83.4 %copy-start = (f32[1024,128]{1,0:T(8,128)S(1)}, f32[1024,128]{1,0:T(8,128)}, u32[]{:S(2)}) copy-start(f32[1024,128]{1,0:T(8,128)} %param.17) | copy-start | bytes 1572868
  1.9 9.1 %all-to-all-start = ((f32[4,1,1]{2,1,0:T(1,128)}), f32[4,1,1]{2,1,0:T(1,128)S(1)}, u32[]{:S(2)}, u32[]{:S(2)}) async-start(f32[4,1,1]{2,1,0:T(1,128)} %stack.72), calls=%async_computation | async-start | bytes 4096 | tf_op jit(solution)/shard_map/all_to_all | solution.py:29
  11.8 15.7 %all-to-all-start.1 = ((f32[8,4,1]{1,2,0:T(1,128)}), f32[8,4,1]{1,2,0:T(1,128)S(1)}, u32[]{:S(2)}, u32[]{:S(2)}) async-start(f32[8,4,1]{1,2,0:T(1,128)} %stack.73), calls=%async_computation.1 | async-start | bytes 8192 | tf_op jit(solution)/shard_map/all_to_all | solution.py:29
  28.0 8.4 all-to-all-start.6
  37.6 8.5 all-to-all-start.10
  43.0 39.4 %copy-start.7 = (s32[64]{0:T(128)S(1)}, s32[64]{0:T(128)}, u32[]{:S(2)}) copy-start(s32[64]{0:T(128)} %param.18) | copy-start | bytes 772
  46.1 11.0 %all-to-all-start.7 = ((f32[8,1,256]{2,1,0:T(1,128)}), f32[8,1,256]{2,1,0:T(1,128)S(1)}, u32[]{:S(2)}, u32[]{:S(2)}) async-start(f32[8,1,256]{2,1,0:T(1,128)} %reshape.971), calls=%async_computation.7 | async-start | bytes 16384 | tf_op jit(solution)/shard_map/all_to_all | solution.py:29
  49.5 33.5 %copy-start.5 = (s32[64,16]{0,1:T(8,128)S(1)}, s32[64,16]{0,1:T(8,128)}, u32[]{:S(2)}) copy-start(s32[64,16]{0,1:T(8,128)} %param.19) | copy-start | bytes 12292
  57.8 11.0 %all-to-all-start.11 = ((f32[8,4,1,128]{3,1,2,0:T(4,128)}), f32[8,4,1,128]{3,1,2,0:T(4,128)S(1)}, u32[]{:S(2)}, u32[]{:S(2)}) async-start(f32[8,4,1,128]{3,1,2,0:T(4,128)} %stack.82), calls=%async_computation.11 | async-start | bytes 32768 | tf_op jit(solution)/shard_map/all_to_all | solution.py:29
  78.1 25.1 %all-to-all-start.4 = ((f32[8,4,1,64,128]{4,3,1,2,0:T(8,128)}), f32[8,4,1,64,128]{4,3,1,2,0:T(8,128)}, u32[]{:S(2)}, u32[]{:S(2)}) async-start(f32[8,4,1,64,128]{4,3,1,2,0:T(8,128)} %stack.76), calls=%async_computation.4 | async-start | bytes 2097152 | tf_op jit(solution)/shard_map/all_to_all | solution.py:29
  103.3 6.4 all-to-all-start.2
  123.7 57.8 %all-to-all-start.9 = ((f32[64,1,64,128]{3,2,1,0:T(8,128)}), f32[64,1,64,128]{3,2,1,0:T(8,128)}, u32[]{:S(2)}, u32[]{:S(2)}) async-start(f32[64,1,64,128]{3,2,1,0:T(8,128)} %fusion.48), calls=%async_computation.9 | async-start | bytes 4194304 | tf_op jit(solution)/shard_map/all_to_all | solution.py:113
  276.7 9.8 %all-to-all-start.13 = ((f32[4,2,256]{2,1,0:T(2,128)}), f32[4,2,256]{2,1,0:T(2,128)S(1)}, u32[]{:S(2)}, u32[]{:S(2)}) async-start(f32[4,2,256]{2,1,0:T(2,128)} %broadcast_in_dim.201), calls=%async_computation.13 | async-start | bytes 16384 | tf_op jit(solution)/shard_map/all_to_all | solution.py:43
  344.5 16.4 %all-to-all-start.14 = ((f32[64,1,128]{2,1,0:T(1,128)}), f32[64,1,128]{2,1,0:T(1,128)S(1)}, u32[]{:S(2)}, u32[]{:S(2)}) async-start(f32[64,1,128]{2,1,0:T(1,128)} %bitcast.70), calls=%async_computation.14 | async-start | bytes 65536 | tf_op jit(solution)/shard_map/all_to_all | solution.py:83
  358.4 23.1 %copy-start.6 = (f32[1,128]{1,0:T(1,128)S(1)}, f32[1,128]{1,0:T(1,128)}, u32[]{:S(2)}) copy-start(f32[1,128]{1,0:T(1,128)} %param.20) | copy-start | bytes 1540
  361.5 14.6 %all-to-all-start.17 = ((f32[8,4,1]{1,2,0:T(1,128)}), f32[8,4,1]{1,2,0:T(1,128)S(1)}, u32[]{:S(2)}, u32[]{:S(2)}) async-start(f32[8,4,1]{1,2,0:T(1,128)} %stack.85), calls=%async_computation.17 | async-start | bytes 8192 | tf_op jit(solution)/shard_map/all_to_all | solution.py:29
  376.1 13.9 %all-to-all-start.20 = ((f32[64,1,64]{2,1,0:T(1,128)}), f32[64,1,64]{2,1,0:T(1,128)S(1)}, u32[]{:S(2)}, u32[]{:S(2)}) async-start(f32[64,1,64]{2,1,0:T(1,128)} %copy.290), calls=%async_computation.20 | async-start | bytes 65536 | tf_op jit(solution)/shard_map/all_to_all | solution.py:83
  390.6 12.4 %all-to-all-start.27 = ((f32[4,1,1,128]{3,2,1,0:T(1,128)}), f32[4,1,1,128]{3,2,1,0:T(1,128)S(1)}, u32[]{:S(2)}, u32[]{:S(2)}) async-start(f32[4,1,1,128]{3,2,1,0:T(1,128)} %stack.93), calls=%async_computation.27 | async-start | bytes 4096 | tf_op jit(solution)/shard_map/all_to_all | solution.py:29
  399.5 7.4 copy-start.3
  403.6 11.5 %all-to-all-start.28 = ((f32[8,4,1,128]{3,1,2,0:T(4,128)}), f32[8,4,1,128]{3,1,2,0:T(4,128)S(1)}, u32[]{:S(2)}, u32[]{:S(2)}) async-start(f32[8,4,1,128]{3,1,2,0:T(4,128)} %stack.94), calls=%async_computation.28 | async-start | bytes 32768 | tf_op jit(solution)/shard_map/all_to_all | solution.py:29
  415.1 62.3 %all-to-all-start.19 = ((f32[64,1,64,128]{3,2,1,0:T(8,128)}), f32[64,1,64,128]{3,2,1,0:T(8,128)S(1)}, u32[]{:S(2)}, u32[]{:S(2)}) async-start(f32[64,1,64,128]{3,2,1,0:T(8,128)} %copy.284), calls=%async_computation.19 | async-start | bytes 4194304 | tf_op jit(solution)/shard_map/all_to_all | solution.py:83
  502.8 8.6 all-to-all-start.24
  512.1 11.0 %all-to-all-start.25 = ((f32[8,1,256]{2,1,0:T(1,128)}), f32[8,1,256]{2,1,0:T(1,128)S(1)}, u32[]{:S(2)}, u32[]{:S(2)}) async-start(f32[8,1,256]{2,1,0:T(1,128)} %reshape.975), calls=%async_computation.25 | async-start | bytes 16384 | tf_op jit(solution)/shard_map/all_to_all | solution.py:29
  523.1 4.5 all-to-all-start.18
  544.5 31.8 %all-to-all-start.22 = ((f32[8,4,1,64,128]{4,3,1,2,0:T(8,128)}), f32[8,4,1,64,128]{4,3,1,2,0:T(8,128)S(1)}, u32[]{:S(2)}, u32[]{:S(2)}) async-start(f32[8,4,1,64,128]{4,3,1,2,0:T(8,128)} %stack.88), calls=%async_computation.22 | async-start | bytes 2097152 | tf_op jit(solution)/shard_map/all_to_all | solution.py:29
  595.9 3.4 copy-start.2
  705.4 8.7 all-to-all-start.30
  750.4 17.7 %all-to-all-start.32 = ((f32[64,1,1]{2,1,0:T(1,128)}), f32[64,1,1]{2,1,0:T(1,128)S(1)}, u32[]{:S(2)}, u32[]{:S(2)}) async-start(f32[64,1,1]{2,1,0:T(1,128)} %all_to_all.149), calls=%async_computation.32 | async-start | bytes 65536 | tf_op jit(solution)/shard_map/all_to_all | solution.py:83
  768.1 19.0 %all-to-all-start.34 = ((f32[64,1,64]{2,1,0:T(1,128)}), f32[64,1,64]{2,1,0:T(1,128)S(1)}, u32[]{:S(2)}, u32[]{:S(2)}) async-start(f32[64,1,64]{2,1,0:T(1,128)} %copy.319), calls=%async_computation.34 | async-start | bytes 65536 | tf_op jit(solution)/shard_map/all_to_all | solution.py:83
  782.7 13.8 %copy-start.4 = (f32[64,64,64]{0,2,1:T(8,128)S(1)}, f32[64,64,64]{0,2,1:T(8,128)}, u32[]{:S(2)}) copy-start(f32[64,64,64]{0,2,1:T(8,128)} %select_add_fusion) | copy-start | bytes 3145732
  787.1 18.0 %all-to-all-start.31 = ((f32[64,1,128]{2,1,0:T(1,128)}), f32[64,1,128]{2,1,0:T(1,128)S(1)}, u32[]{:S(2)}, u32[]{:S(2)}) async-start(f32[64,1,128]{2,1,0:T(1,128)} %bitcast.115), calls=%async_computation.31 | async-start | bytes 65536 | tf_op jit(solution)/shard_map/all_to_all | solution.py:83
  805.1 61.4 %all-to-all-start.33 = ((f32[64,1,64,128]{3,2,1,0:T(8,128)}), f32[64,1,64,128]{3,2,1,0:T(8,128)S(1)}, u32[]{:S(2)}, u32[]{:S(2)}) async-start(f32[64,1,64,128]{3,2,1,0:T(8,128)} %copy.313), calls=%async_computation.33 | async-start | bytes 4194304 | tf_op jit(solution)/shard_map/all_to_all | solution.py:83
  815.3 75.8 %copy-start.1 = (f32[1024,128]{1,0:T(8,128)S(1)}, f32[1024,128]{1,0:T(8,128)}, u32[]{:S(2)}) copy-start(f32[1024,128]{1,0:T(8,128)} %param.17) | copy-start | bytes 1572868
